TPU v7x, 16 devices: a 4x2x1 block of a 4x4x4 slice. The times are simulated.
16 devices in a mesh: dp: 4 (over y, z, core), tp: 4 (over x).
Axes of the slice: x: 4, y: 2, z: 1, core: 2. Of those that a mesh axis runs over, the one named last changes fastest.
The devices are a block of a 4x4x4 slice.
Arguments:
- x: bfloat16 [2560, 7168], P(('dp', 'tp')), parts along dimension 0
- dy: bfloat16 [2560, 7168], P(('dp', 'tp')), parts along dimension 0
- pre: bfloat16 [2560, 28672], P('dp', 'tp'), parts along dimension 0
- w_in: bfloat16 [7168, 28672], P(None, 'tp')
- w_down: bfloat16 [28672, 7168], P('tp')
Outputs:
- output 1: bfloat16 [2560, 7168], P(('dp', 'tp')), parts along dimension 0
- output 2: bfloat16 [28672, 28672], P('dp', 'tp'), parts along dimension 0
- output 3: bfloat16 [114688, 7168], P(('dp', 'tp')), parts along dimension 0
There are 4 independent parts. A program takes and returns all parts, laid end to end along the dimension named above; an argument that names none is the same for every part.
All inputs are finite; a program needn't handle non-finite values.
Results may differ from a plain program's by a relative error of at most 0.012.
Values are sent between devices in bfloat16 or wider.
A program may use at most 1.5 GiB of HBM per device.

v0:
```python
import jax
import jax.numpy as jnp


def act(pre):
    return jax.nn.gelu(pre)


def solution(mesh):
    def step(x, dy, pre, w_in, w_down):
        hidden, back = jax.vjp(act, pre.astype(jnp.float32))
        d_hidden = jnp.dot(dy, w_down.T, preferred_element_type=jnp.float32)
        d_pre = back(d_hidden)[0].astype(jnp.bfloat16)
        dx = jnp.dot(d_pre, w_in.T)
        groups = mesh.shape["dp"]

        def by_group(a, b):
            a, b = (t.reshape(groups, -1, t.shape[-1]) for t in (a, b))
            product = jnp.einsum("gta,gtb->gab", a, b, preferred_element_type=jnp.float32)
            return product.astype(jnp.bfloat16).reshape(-1, b.shape[-1])

        return dx, by_group(x, d_pre), by_group(hidden.astype(jnp.bfloat16), dy)

    return step
```

profile of v0, /device:TPU:112, one launch (start us, length us, event | category | flops | bytes accessed | tf_op | source)
XLA Modules:
  0.0 851.5 jit_solution(3958592969454872633)
XLA Ops:
  7.2 0.1 all-gather.5.cloned.1.call-start
  7.2 0.7 all-gather.5.cloned.1.call-update
  8.0 0.1 reduce-scatter.4.cloned.1.call-start
  8.0 2.4 collective-permute-start
  10.5 1.6 collective-permute-start.1
  12.1 1.6 collective-permute-start.2
  13.7 0.4 collective-permute-start.4
  14.1 1.2 dynamic-slice.30
  18.0 83.0 %collective-permute-done = bf16[1,1,160,7168]{3,2,1,0:T(8,128)(2,1)} collective-permute-done((bf16[1,1,160,7168]{3,2,1,0:T(8,128)(2,1)}, bf16[1,1,160,7168]{3,2,1,0:T(8,128)(2,1)}, u32[]{:S(2)}, u32[]{:S(2)}) %collective-permute-start) | collective-permute-done | bytes 2293792 | tf_op jit(solution)/gta,gtb->gab/dot_general | solution.py:19
  100.9 1.9 collective-permute-start.3
  102.8 82.8 %collective-permute-done.1 = bf16[1,1,160,7168]{3,2,1,0:T(8,128)(2,1)} collective-permute-done((bf16[1,1,160,7168]{3,2,1,0:T(8,128)(2,1)}, bf16[1,1,160,7168]{3,2,1,0:T(8,128)(2,1)}, u32[]{:S(2)}, u32[]{:S(2)}) %collective-permute-start.1) | collective-permute-done | bytes 2293792 | tf_op jit(solution)/gta,gtb->gab/dot_general | solution.py:19
  185.6 0.5 collective-permute-start.5
  186.1 0.0 all-gather.5.cloned.1.call-done
  186.1 86.6 %fusion.13 = (bf16[1,1,640,7168]{3,2,1,0:T(8,128)(2,1)}, bf16[640,7168]{1,0:T(8,128)(2,1)S(1)}) fusion(bf16[640,7168]{1,0:T(8,128)(2,1)} %param.6, bf16[640,7168]{1,0:T(8,128)(2,1)} %all-gather.5.cloned.1.call-done, bf16[7168,7168]{1,0:T(8,128)(2,1)} %param.5), kind=kOutput, calls=%fused_computation.28 | convolution fusion | flops 65872199680 | bytes 139460608 | tf_op jit(solution)/dot_general | solution.py:12
  272.7 0.0 copy-start.2
  272.7 3.7 copy-done.2
  276.3 73.1 %fusion.44 = bf16[640,7168]{1,0:T(8,128)(2,1)} fusion(bf16[640,7168]{1,0:T(8,128)(2,1)S(1)} %get-tuple-element.28, bf16[7168,7168]{1,0:T(8,128)(2,1)} %param.7), kind=kOutput, calls=%fused_computation.59 | convolution fusion | flops 65766686720 | bytes 121110528 | tf_op jit(solution)/dot_general | solution.py:14
  349.4 0.0 copy-start.1
  349.4 0.1 reduce-scatter.4.cloned.1.call-update
  349.5 1.6 copy-done.1
  351.1 72.6 %fusion.16 = f32[7168,7168,1]{1,0,2:T(8,128)} fusion(s32[]{:T(128)} %bitcast.2, bf16[1,1,640,7168]{3,2,1,0:T(8,128)(2,1)} %bitcast.94, s32[]{:T(128)} %bitcast.3, bf16[1,1,160,7168]{3,2,1,0:T(8,128)(2,1)} %collective-permute-done, bf16[1,1,160,7168]{3,2,1,0:T(8,128)(2,1)S(1)} %bitcast.93), kind=kOutput, calls=%fused_computation.31 | convolution fusion | flops 32894812160 | bytes 219283456 | tf_op jit(solution)/gta,gtb->gab/dot_general | solution.py:19
  423.7 0.0 collective-permute-done.2
  423.7 0.0 collective-permute-done.3
  423.7 0.0 copy-start
  423.7 107.8 %fusion.2 = bf16[7168,7168]{0,1:T(8,128)(2,1)} fusion(f32[7168,7168,1]{1,0,2:T(8,128)} %fusion.16, s32[]{:T(128)} %bitcast.8, bf16[1,1,640,7168]{3,2,1,0:T(8,128)(2,1)} %bitcast.95, s32[]{:T(128)} %bitcast.9, bf16[1,1,160,7168]{3,2,1,0:T(8,128)(2,1)} %collective-permute-done.3, bf16[1,1,160,7168]{3,2,1,0:T(8,128)(2,1)} %collective-permute-done.2), kind=kOutput, calls=%fused_computation.4 | convolution fusion | flops 32997572608 | bytes 322043904 | tf_op jit(solution)/gta,gtb->gab/dot_general | solution.py:19
  531.5 0.0 copy-done
  531.5 72.8 %fusion.23 = f32[7168,7168,1]{1,0,2:T(8,128)} fusion(s32[]{:T(128)} %bitcast.2, bf16[1,1,640,7168]{3,2,1,0:T(8,128)(2,1)} %get-tuple-element.27, s32[]{:T(128)} %bitcast.3, bf16[1,1,160,7168]{3,2,1,0:T(8,128)(2,1)} %collective-permute-done.1, bf16[1,1,160,7168]{3,2,1,0:T(8,128)(2,1)S(1)} %bitcast.90), kind=kOutput, calls=%fused_computation.36 | convolution fusion | flops 32894812160 | bytes 219283456 | tf_op jit(solution)/gta,gtb->gab/dot_general | solution.py:19
  604.3 132.7 %copy = bf16[7168,7168]{1,0:T(8,128)(2,1)} copy(bf16[7168,7168]{0,1:T(8,128)(2,1)} %fusion.2) | data formatting | bytes 205520896
  736.9 0.0 collective-permute-done.4
  736.9 0.0 collective-permute-done.5
  736.9 107.7 %fusion = bf16[7168,7168]{1,0:T(8,128)(2,1)} fusion(f32[7168,7168,1]{1,0,2:T(8,128)} %fusion.23, s32[]{:T(128)} %bitcast.8, bf16[1,1,640,7168]{3,2,1,0:T(8,128)(2,1)} %get-tuple-element.27, s32[]{:T(128)} %bitcast.9, bf16[1,1,160,7168]{3,2,1,0:T(8,128)(2,1)} %collective-permute-done.5, bf16[1,1,160,7168]{3,2,1,0:T(8,128)(2,1)} %collective-permute-done.4), kind=kOutput, calls=%fused_computation.1 | convolution fusion | flops 32997572608 | bytes 322043904 | tf_op jit(solution)/gta,gtb->gab/dot_general | solution.py:19
  844.7 0.0 reduce-scatter.4.cloned.1.call-done
Async XLA Ops:
  7.2 178.9 %all-gather.5.cloned.1.call-start = ((), (), s32[]{:S(2)}) async-start(), calls=%async_computation.1 | async-start | bytes 11468800 | tf_op args[1]
  8.0 836.7 %reduce-scatter.4.cloned.1.call-start = ((), (), s32[]{:S(2)}) async-start(), calls=%async_computation.2 | async-start | bytes 11468800
  8.0 92.9 %collective-permute-start = (bf16[1,1,160,7168]{3,2,1,0:T(8,128)(2,1)}, bf16[1,1,160,7168]{3,2,1,0:T(8,128)(2,1)}, u32[]{:S(2)}, u32[]{:S(2)}) collective-permute-start(bf16[1,1,160,7168]{3,2,1,0:T(8,128)(2,1)} %bitcast.91), channel_id=5, source_target_pairs={{0,1},{1,2},{2,3},{3,0},{4,5},{5,6},{6,7},{7,4},{8,9},{9,10},{10,1... | collective-permute-start | bytes 6881288 | tf_op jit(solution)/gta,gtb->gab/dot_general | solution.py:19
  10.5 175.1 %collective-permute-start.1 = (bf16[1,1,160,7168]{3,2,1,0:T(8,128)(2,1)}, bf16[1,1,160,7168]{3,2,1,0:T(8,128)(2,1)}, u32[]{:S(2)}, u32[]{:S(2)}) collective-permute-start(bf16[1,1,160,7168]{3,2,1,0:T(8,128)(2,1)} %bitcast.88), channel_id=11, source_target_pairs={{0,1},{1,2},{2,3},{3,0},{4,5},{5,6},{6,7},{7,4},{8,9},{9,10},{10,1... | collective-permute-start | bytes 6881288 | tf_op jit(solution)/gta,gtb->gab/dot_general | solution.py:19
  12.1 411.6 %collective-permute-start.2 = (bf16[1,1,160,7168]{3,2,1,0:T(8,128)(2,1)}, bf16[1,1,160,7168]{3,2,1,0:T(8,128)(2,1)}, u32[]{:S(2)}, u32[]{:S(2)}) collective-permute-start(bf16[1,1,160,7168]{3,2,1,0:T(8,128)(2,1)} %bitcast.92), channel_id=6, source_target_pairs={{0,3},{1,0},{2,1},{3,2},{4,7},{5,4},{6,5},{7,6},{8,11},{9,8},{10,9... | collective-permute-start | bytes 6881288 | tf_op jit(solution)/gta,gtb->gab/dot_general | solution.py:19
  13.7 723.2 %collective-permute-start.4 = (bf16[1,1,160,7168]{3,2,1,0:T(8,128)(2,1)}, bf16[1,1,160,7168]{3,2,1,0:T(8,128)(2,1)}, u32[]{:S(2)}, u32[]{:S(2)}) collective-permute-start(bf16[1,1,160,7168]{3,2,1,0:T(8,128)(2,1)} %bitcast.89), channel_id=12, source_target_pairs={{0,3},{1,0},{2,1},{3,2},{4,7},{5,4},{6,5},{7,6},{8,11},{9,8},{10,9... | collective-permute-start | bytes 6881288 | tf_op jit(solution)/gta,gtb->gab/dot_general | solution.py:19
  100.9 322.7 %collective-permute-start.3 = (bf16[1,1,160,7168]{3,2,1,0:T(8,128)(2,1)}, bf16[1,1,160,7168]{3,2,1,0:T(8,128)(2,1)}, u32[]{:S(2)}, u32[]{:S(2)}) collective-permute-start(bf16[1,1,160,7168]{3,2,1,0:T(8,128)(2,1)} %collective-permute-done), channel_id=7, source_target_pairs={{0,1},{1,2},{2,3},{3,0},{4,5},{5,6},{6,7},{7,4},{8,9},{9,10},{10,1... | collective-permute-start | bytes 6881288 | tf_op jit(solution)/gta,gtb->gab/dot_general | solution.py:19
  185.6 551.3 %collective-permute-start.5 = (bf16[1,1,160,7168]{3,2,1,0:T(8,128)(2,1)}, bf16[1,1,160,7168]{3,2,1,0:T(8,128)(2,1)}, u32[]{:S(2)}, u32[]{:S(2)}) collective-permute-start(bf16[1,1,160,7168]{3,2,1,0:T(8,128)(2,1)} %collective-permute-done.1), channel_id=13, source_target_pairs={{0,1},{1,2},{2,3},{3,0},{4,5},{5,6},{6,7},{7,4},{8,9},{9,10},{10,1... | collective-permute-start | bytes 6881288 | tf_op jit(solution)/gta,gtb->gab/dot_general | solution.py:19
  272.7 3.7 copy-start.2
  349.4 1.6 copy-start.1
  423.7 107.8 %copy-start = (bf16[160,7168]{1,0:T(8,128)(2,1)S(1)}, bf16[160,7168]{1,0:T(8,128)(2,1)}, u32[]{:S(2)}) copy-start(bf16[160,7168]{1,0:T(8,128)(2,1)} %param.4) | copy-start | bytes 6881284
Sparse Core Ops, SparseCore 0:
  9.6 162.8 all-gather.4
  349.6 84.6 reduce-scatter.3
where the time goes:
time: 855 us; the launch traced here: 852 us
  matrix products  521 us (61%)
  waiting for transfers between devices  167 us (20%)
  local copies, waits for them, and re-layouts  139 us (16%)
  between operations  16.7 us (2%)
  starting transfers between devices  8.56 us (1%)
    dot_general x4, matrix products, by_group(): jnp.einsum('gta,gtb->gab', a, b, preferred_element_type=jnp.float32)  361 us
    dot_general x6, waiting for transfers between devices, by_group(): jnp.einsum('gta,gtb->gab', a, b, preferred_element_type=jnp.float32)  166 us
    unnamed x7, local copies, waits for them, and re-layouts  138 us
    dot_general x1, matrix products, step(): d_hidden = jnp.dot(dy, w_down.T, preferred_element_type=jnp.float32)  86.6 us
    dot_general x1, matrix products, step(): dx = jnp.dot(d_pre, w_in.T)  73.1 us
  transfers between devices with their start and end apart: 8, of which 2 were waited for; matrix products, arithmetic and copies ran while one was open for 77% of the time, Pallas kernels for 0%

commit v1 on v0

v1 whole, which is shorter than its diff:
```python
import functools

import jax
import jax.numpy as jnp
from jax import lax
from jax.experimental import pallas as pl
from jax.experimental.pallas import tpu as pltpu
from jax.sharding import PartitionSpec as P

VMEM_LIMIT = 60 * 1024 * 1024


def act(pre):
    return jax.nn.gelu(pre)


def params(n=1):
    return pltpu.CompilerParams(
        dimension_semantics=("arbitrary",) * n, vmem_limit_bytes=VMEM_LIMIT
    )


def whole(shape):
    return pl.BlockSpec(shape, lambda *i: (0,) * len(shape), pipeline_mode=pl.Buffered(1))


def gelu_kernel(pre_ref, hidden_ref, slope_ref):
    hidden, back = jax.vjp(act, pre_ref[...].astype(jnp.float32))
    slope_ref[...] = back(jnp.ones_like(hidden))[0]
    hidden_ref[...] = hidden.astype(jnp.bfloat16).T


def gelu_pass(pre, tile):
    rows, cols = pre.shape
    return pl.pallas_call(
        gelu_kernel,
        grid=(cols // tile,),
        in_specs=[pl.BlockSpec((rows, tile), lambda i: (0, i))],
        out_specs=[
            pl.BlockSpec((tile, rows), lambda i: (i, 0)),
            pl.BlockSpec((rows, tile), lambda i: (0, i)),
        ],
        out_shape=[
            jax.ShapeDtypeStruct((cols, rows), jnp.bfloat16),
            jax.ShapeDtypeStruct((rows, cols), jnp.float32),
        ],
        compiler_params=params(),
        cost_estimate=pl.CostEstimate(
            flops=30 * rows * cols, bytes_accessed=8 * rows * cols, transcendentals=rows * cols
        ),
        name="gelu",
    )(pre)


def down_kernel(hidden_ref, dy_ref, *refs):
    out_ref = refs[-1]
    out_ref[...] = jnp.dot(
        hidden_ref[...], dy_ref[...], preferred_element_type=jnp.float32
    ).astype(out_ref.dtype)


def down_pass(hidden_t, dy, into, start, cols, tile):
    m, k = hidden_t.shape
    n = dy.shape[1]
    at = start // n
    args, specs, alias = [hidden_t, dy], [
        pl.BlockSpec((tile, k), lambda i: (i, 0)),
        whole((k, n)),
    ], {}
    if into is not None:
        args.append(into)
        specs.append(pl.BlockSpec(memory_space=pl.ANY))
        alias = {2: 0}
    return pl.pallas_call(
        down_kernel,
        grid=(m // tile,),
        in_specs=specs,
        out_specs=pl.BlockSpec((tile, n), lambda i: (i, at)),
        out_shape=jax.ShapeDtypeStruct((m, cols), jnp.bfloat16),
        input_output_aliases=alias,
        compiler_params=params(),
        cost_estimate=pl.CostEstimate(
            flops=2 * m * k * n, bytes_accessed=2 * (m * k + k * n + m * n), transcendentals=0
        ),
        name="dw_down",
    )(*args)


def pre_kernel(parts, *refs):
    dys, (w_ref, slope_ref, out_ref) = refs[:parts], refs[parts:]
    total, at = None, 0
    for dy_ref in dys:
        n = dy_ref.shape[1]
        term = lax.dot_general(
            dy_ref[...],
            w_ref[:, at : at + n],
            (((1,), (1,)), ((), ())),
            preferred_element_type=jnp.float32,
        )
        total = term if total is None else total + term
        at += n
    out_ref[...] = (total * slope_ref[...]).astype(out_ref.dtype)


def pre_pass(dys, w, slope, tile):
    rows = dys[0].shape[0]
    n, k = w.shape
    return pl.pallas_call(
        functools.partial(pre_kernel, len(dys)),
        grid=(n // tile,),
        in_specs=[whole(d.shape) for d in dys]
        + [
            pl.BlockSpec((tile, k), lambda i: (i, 0)),
            pl.BlockSpec((rows, tile), lambda i: (0, i)),
        ],
        out_specs=pl.BlockSpec((rows, tile), lambda i: (0, i)),
        out_shape=jax.ShapeDtypeStruct((rows, n), jnp.bfloat16),
        compiler_params=params(),
        cost_estimate=pl.CostEstimate(
            flops=2 * rows * n * k, bytes_accessed=2 * (rows * k + n * k + 3 * rows * n), transcendentals=0
        ),
        name="d_pre",
    )(*dys, w, slope)


def dx_kernel(d_ref, w_ref, out_ref):
    out_ref[...] = lax.dot_general(
        d_ref[...], w_ref[...], (((1,), (1,)), ((), ())), preferred_element_type=jnp.float32
    ).astype(out_ref.dtype)


def dx_pass(d_pre, w, start, cols, tile):
    rows, k = d_pre.shape
    at = start // tile
    return pl.pallas_call(
        dx_kernel,
        grid=(cols // tile,),
        in_specs=[whole((rows, k)), pl.BlockSpec((tile, k), lambda i: (i + at, 0))],
        out_specs=pl.BlockSpec((rows, tile), lambda i: (0, i)),
        out_shape=jax.ShapeDtypeStruct((rows, cols), jnp.bfloat16),
        compiler_params=params(),
        cost_estimate=pl.CostEstimate(
            flops=2 * rows * cols * k, bytes_accessed=2 * (rows * k + cols * k + rows * cols), transcendentals=0
        ),
        name="dx",
    )(d_pre, w)


def in_kernel(x_ref, d_ref, out_ref):
    out_ref[...] = lax.dot_general(
        x_ref[...], d_ref[...], (((0,), (0,)), ((), ())), preferred_element_type=jnp.float32
    ).astype(out_ref.dtype)


def in_pass(x, d_pre, tile):
    rows, m = x.shape
    n = d_pre.shape[1]
    return pl.pallas_call(
        in_kernel,
        grid=(m // tile,),
        in_specs=[pl.BlockSpec((rows, tile), lambda i: (0, i)), whole((rows, n))],
        out_specs=pl.BlockSpec((tile, n), lambda i: (i, 0)),
        out_shape=jax.ShapeDtypeStruct((m, n), jnp.bfloat16),
        compiler_params=params(),
        cost_estimate=pl.CostEstimate(
            flops=2 * rows * m * n, bytes_accessed=2 * (rows * m + rows * n + m * n), transcendentals=0
        ),
        name="dw_in",
    )(x, d_pre)


PARTS = 4
HALVES = 2


def solution(mesh):
    def step(x, dy, pre, w_in, w_down):
        d = dy.shape[1]
        part = d // PARTS
        gather = functools.partial(lax.all_gather, axis_name="tp", axis=0, tiled=True)
        dys = [gather(dy[:, i * part : (i + 1) * part]) for i in range(PARTS)]
        hidden_t, slope = gelu_pass(pre, 512)
        x, dys[-1] = lax.optimization_barrier((x, dys[-1]))
        x_all = gather(x)
        dw_down = None
        for i in range(PARTS):
            dw_down = down_pass(hidden_t, dys[i], dw_down, i * part, d, 1024)
        dys, dw_down = lax.optimization_barrier((dys, dw_down))
        d_pre = pre_pass(dys, w_down, slope, 512)
        half = w_in.shape[0] // HALVES
        dx = []
        for i in range(HALVES):
            term = dx_pass(d_pre, w_in, i * half, half, 512)
            dx.append(lax.psum_scatter(term, "tp", scatter_dimension=0, tiled=True))
        dw_in = in_pass(x_all, d_pre, 512)
        return jnp.concatenate(dx, axis=1), dw_in, dw_down

    return jax.shard_map(
        step,
        mesh=mesh,
        in_specs=(
            P(("dp", "tp"), None),
            P(("dp", "tp"), None),
            P("dp", "tp"),
            P(None, "tp"),
            P("tp", None),
        ),
        out_specs=(P(("dp", "tp"), None), P("dp", "tp"), P(("dp", "tp"), None)),
        check_vma=False,
    )
```

time: 855 us -> 578 us (0.68)
  matrix products: 521 us -> 0 us
  Pallas kernels: 0 us -> 369 us
  local copies, waits for them, and re-layouts: 139 us -> 2.99 us
  waiting for transfers between devices: 167 us -> 188 us
    dot_general x6 -> x0, matrix products: 521 us -> none  [the longest x4 361 us: by_group(): jnp.einsum('gta,gtb->gab', a, b, preferred_element_type=jnp.float32)]
    pallas_call x0 -> x9, Pallas kernels: none -> 369 us  [the longest x4 100 us: down_pass(): pl.pallas_call(down_kernel, grid=(m // tile,), in_specs=specs, out_specs=...]
    dot_general x6 -> x0, waiting for transfers between devices: 166 us -> none  [by_group(): jnp.einsum('gta,gtb->gab', a, b, preferred_element_type=jnp.float32)]
    unnamed x7 -> x0, local copies, waits for them, and re-layouts: 138 us -> none
    all_gather x0 -> x5, waiting for transfers between devices: none -> 132 us  [the longest x1 84 us: step(): x_all = gather(x)]
    reduce_scatter x0 -> x2, waiting for transfers between devices: none -> 52.7 us  [step(): dx.append(lax.psum_scatter(term, 'tp', scatter_dimension=0, tiled=True))]
  transfers between devices with their start and end apart: 8 -> 7, of which waited for: 2 -> 7; matrix products, arithmetic and copies ran while one was open for 77% -> 1% of each run, Pallas kernels for 0% -> 19%
where the time goes in v1:
time: 578 us; the launch traced here: 577 us
  Pallas kernels  369 us (64%)
  waiting for transfers between devices  188 us (33%)
  between operations  14.2 us (2%)
    pallas_call x4, Pallas kernels, down_pass(): pl.pallas_call(down_kernel, grid=(m // tile,), in_specs=specs, out_specs=...  100 us
    pallas_call x1, Pallas kernels, in_pass(): pl.pallas_call(in_kernel, grid=(m // tile,), in_specs=[pl.BlockSpec((rows...  89.6 us
    all_gather x1, waiting for transfers between devices, step(): x_all = gather(x)  84 us
    pallas_call x2, Pallas kernels, dx_pass(): pl.pallas_call(dx_kernel, grid=(cols // tile,), in_specs=[whole((rows, k)...  82.2 us
    pallas_call x1, Pallas kernels, pre_pass(): pl.pallas_call(functools.partial(pre_kernel, len(dys)), grid=(n // tile,)...  76.2 us
    reduce_scatter x2, waiting for transfers between devices, step(): dx.append(lax.psum_scatter(term, 'tp', scatter_dimension=0, tiled=True))  52.7 us
    all_gather x4, waiting for transfers between devices, step(): dys = [gather(dy[:, i * part:(i + 1) * part]) for i in range(PARTS)]  48 us
    pallas_call x1, Pallas kernels, gelu_pass(): pl.pallas_call(gelu_kernel, grid=(cols // tile,), in_specs=[pl.BlockSpec(...  20.1 us
  transfers between devices with their start and end apart: 7, of which 7 were waited for; matrix products, arithmetic and copies ran while one was open for 1% of the time, Pallas kernels for 19%

profile of v1, /device:TPU:112, one launch (start us, length us, event | category | flops | bytes accessed | tf_op | source)
XLA Modules:
  0.0 577.0 jit_solution(11990860839194548900)
XLA Ops:
  7.2 0.1 all-gather.12.cloned.1.call-start
  7.2 3.0 fusion
  10.2 0.1 all-gather.12.cloned.1.call-update
  10.3 0.1 all-gather.6.cloned.1.call-start
  10.4 0.7 all-gather.6.cloned.1.call-update
  11.1 0.1 all-gather.8.cloned.1.call-start
  11.2 0.7 all-gather.8.cloned.1.call-update
  11.9 0.1 all-gather.10.cloned.1.call-start
  12.0 0.6 all-gather.10.cloned.1.call-update
  12.5 0.1 reduce-scatter.3.cloned.1.call-start
  12.6 20.1 %gelu.1 = (bf16[7168,640]{1,0:T(8,128)(2,1)}, f32[640,7168]{1,0:T(8,128)}) custom-call(bf16[640,7168]{1,0:T(8,128)(2,1)} %pre_ref.1), custom_call_target="tpu_custom_call" | custom-call | flops 137625600 | bytes 36700160 | tf_op jit(solution)/shard_map/gelu/pallas_call | solution.py:35
  32.7 8.6 %all-gather.12.cloned.1.call-done.dy_ref.refs_3_ = bf16[640,1792]{1,0:T(8,128)(2,1)} async-done(((bf16[160,1792]{1,0:T(8,128)(2,1)}), bf16[640,1792]{1,0:T(8,128)(2,1)}) %all-gather.12.cloned.1.call-update) | async-done | bytes 2293776 | tf_op jit(solution)/shard_map/all_gather | solution.py:181
  41.3 30.3 %all-gather.6.cloned.1.call-done.dy_ref.refs_0_ = bf16[640,1792]{1,0:T(8,128)(2,1)} async-done(((bf16[160,1792]{1,0:T(8,128)(2,1)}), bf16[640,1792]{1,0:T(8,128)(2,1)}) %all-gather.6.cloned.1.call-update) | async-done | bytes 2293776 | tf_op jit(solution)/shard_map/all_gather | solution.py:181
  71.6 25.1 %dw_down.4.refs_0_ = bf16[7168,7168]{1,0:T(8,128)(2,1)} custom-call(bf16[7168,640]{1,0:T(8,128)(2,1)} %get-tuple-element.13.hidden_ref, bf16[640,1792]{1,0:T(8,128)(2,1)} %all-gather.6.cloned.1.call-done.dy_ref.refs_0_), custom_call_target="tpu_custom_call" | custom-call | flops 16441671680 | bytes 37158912 | tf_op jit(solution)/shard_map/dw_down/pallas_call | solution.py:74
  96.7 4.6 all-gather.8.cloned.1.call-done.dy_ref.refs_1_
  101.3 25.1 %dw_down.5.refs_0_ = bf16[7168,7168]{1,0:T(8,128)(2,1)} custom-call(bf16[7168,640]{1,0:T(8,128)(2,1)} %get-tuple-element.13.hidden_ref, bf16[640,1792]{1,0:T(8,128)(2,1)} %all-gather.8.cloned.1.call-done.dy_ref.refs_1_, bf16[7168,7168]{1,0:T(8,128)(2,1)} %dw_down.4.refs_0_), custom_call_target="tpu_custom_call", output_to_operand_aliasing={{}: (2, {})} | custom-call | flops 16441671680 | bytes 37158912 | tf_op jit(solution)/shard_map/dw_down/pallas_call | solution.py:74
  126.4 4.5 all-gather.10.cloned.1.call-done.dy_ref.refs_2_
  130.9 25.1 %dw_down.6.refs_0_ = bf16[7168,7168]{1,0:T(8,128)(2,1)} custom-call(bf16[7168,640]{1,0:T(8,128)(2,1)} %get-tuple-element.13.hidden_ref, bf16[640,1792]{1,0:T(8,128)(2,1)} %all-gather.10.cloned.1.call-done.dy_ref.refs_2_, bf16[7168,7168]{1,0:T(8,128)(2,1)} %dw_down.5.refs_0_), custom_call_target="tpu_custom_call", output_to_operand_aliasing={{}: (2, {})} | custom-call | flops 16441671680 | bytes 37158912 | tf_op jit(solution)/shard_map/dw_down/pallas_call | solution.py:74
  156.0 25.1 %dw_down.7 = bf16[7168,7168]{1,0:T(8,128)(2,1)} custom-call(bf16[7168,640]{1,0:T(8,128)(2,1)} %get-tuple-element.13.hidden_ref, bf16[640,1792]{1,0:T(8,128)(2,1)} %all-gather.12.cloned.1.call-done.dy_ref.refs_3_, bf16[7168,7168]{1,0:T(8,128)(2,1)} %dw_down.6.refs_0_), custom_call_target="tpu_custom_call", output_to_operand_aliasing={{}: (2, {})} | custom-call | flops 16441671680 | bytes 37158912 | tf_op jit(solution)/shard_map/dw_down/pallas_call | solution.py:74
  181.2 76.2 %d_pre.1.d_ref = bf16[640,7168]{1,0:T(8,128)(2,1)} custom-call(bf16[640,1792]{1,0:T(8,128)(2,1)} %all-gather.6.cloned.1.call-done.dy_ref.refs_0_, bf16[640,1792]{1,0:T(8,128)(2,1)} %all-gather.8.cloned.1.call-done.dy_ref.refs_1_, bf16[640,1792]{1,0:T(8,128)(2,1)} %all-gather.10.cloned.1.call-done.dy_ref.refs_2_, ...), custom_call_target="tpu_custom_call" | custom-call | flops 65766686720 | bytes 139460608 | tf_op jit(solution)/shard_map/d_pre/pallas_call | solution.py:108
  257.4 41.1 %dx.2 = bf16[640,3584]{1,0:T(8,128)(2,1)} custom-call(bf16[640,7168]{1,0:T(8,128)(2,1)} %d_pre.1.d_ref, bf16[7168,7168]{1,0:T(8,128)(2,1)} %w_ref.3), custom_call_target="tpu_custom_call" | custom-call | flops 32883343360 | bytes 65142784 | tf_op jit(solution)/shard_map/dx/pallas_call | solution.py:135
  298.5 0.1 reduce-scatter.3.cloned.1.call-update
  298.6 0.1 reduce-scatter.5.cloned.1.call-start
  298.6 41.1 %dx.3 = bf16[640,3584]{1,0:T(8,128)(2,1)} custom-call(bf16[640,7168]{1,0:T(8,128)(2,1)} %d_pre.1.d_ref, bf16[7168,7168]{1,0:T(8,128)(2,1)} %w_ref.3), custom_call_target="tpu_custom_call" | custom-call | flops 32883343360 | bytes 65142784 | tf_op jit(solution)/shard_map/dx/pallas_call | solution.py:135
  339.8 0.1 reduce-scatter.5.cloned.1.call-update
  339.8 0.1 all-gather.14.cloned.1.call-start
  339.9 0.7 all-gather.14.cloned.1.call-update
  340.6 4.2 reduce-scatter.3.cloned.1.call-done
  344.9 48.5 %reduce-scatter.5.cloned.1.call-done = bf16[160,3584]{1,0:T(8,128)(2,1)} async-done(((bf16[640,3584]{1,0:T(8,128)(2,1)}), bf16[160,3584]{1,0:T(8,128)(2,1)}) %reduce-scatter.5.cloned.1.call-update) | async-done | bytes 1146896 | tf_op jit(solution)/shard_map/reduce_scatter | solution.py:194
  393.3 3.2 pad_maximum_fusion
  396.5 84.0 %all-gather.14.cloned.1.call-done.x_ref = bf16[640,7168]{1,0:T(8,128)(2,1)} async-done(((bf16[160,7168]{1,0:T(8,128)(2,1)}), bf16[640,7168]{1,0:T(8,128)(2,1)}) %all-gather.14.cloned.1.call-update) | async-done | bytes 9175056 | tf_op jit(solution)/shard_map/all_gather | solution.py:184
  480.5 89.6 %dw_in.1 = bf16[7168,7168]{1,0:T(8,128)(2,1)} custom-call(bf16[640,7168]{1,0:T(8,128)(2,1)} %all-gather.14.cloned.1.call-done.x_ref, bf16[640,7168]{1,0:T(8,128)(2,1)} %d_pre.1.d_ref), custom_call_target="tpu_custom_call" | custom-call | flops 65766686720 | bytes 121110528 | tf_op jit(solution)/shard_map/dw_in/pallas_call | solution.py:158
Async XLA Ops:
  7.2 34.1 %all-gather.12.cloned.1.call-start = ((), (), s32[]{:S(2)}) async-start(), calls=%async_computation.5 | async-start | bytes 2867200 | tf_op jit(solution)/shard_map/all_gather | solution.py:181
  10.3 61.3 %all-gather.6.cloned.1.call-start = ((), (), s32[]{:S(2)}) async-start(), calls=%async_computation.2 | async-start | bytes 2867200 | tf_op jit(solution)/shard_map/all_gather | solution.py:181
  11.1 90.2 %all-gather.8.cloned.1.call-start = ((), (), s32[]{:S(2)}) async-start(), calls=%async_computation.3 | async-start | bytes 2867200 | tf_op jit(solution)/shard_map/all_gather | solution.py:181
  11.9 119.0 %all-gather.10.cloned.1.call-start = ((), (), s32[]{:S(2)}) async-start(), calls=%async_computation.4 | async-start | bytes 2867200 | tf_op jit(solution)/shard_map/all_gather | solution.py:181
  12.5 332.3 %reduce-scatter.3.cloned.1.call-start = ((), (), s32[]{:S(2)}) async-start(), calls=%async_computation.6 | async-start | bytes 5734400 | tf_op jit(solution)/shard_map/reduce_scatter | solution.py:194
  298.6 94.8 %reduce-scatter.5.cloned.1.call-start = ((), (), s32[]{:S(2)}) async-start(), calls=%async_computation.7 | async-start | bytes 5734400 | tf_op jit(solution)/shard_map/reduce_scatter | solution.py:194
  339.8 140.7 %all-gather.14.cloned.1.call-start = ((), (), s32[]{:S(2)}) async-start(), calls=%async_computation.8 | async-start | bytes 11468800 | tf_op jit(solution)/shard_map/all_gather | solution.py:184
Sparse Core Ops, SparseCore 0:
  10.4 30.8 all-gather.11
  43.4 28.1 all-gather.5
  73.1 28.1 all-gather.7
  102.7 28.1 all-gather.9
  298.7 46.1 reduce-scatter.2
  347.6 45.6 reduce-scatter.4
  394.9 85.6 all-gather.13
